TPU v7x, 32 devices: a whole 2x2x4 slice. The times are simulated.
32 devices in a mesh: groups: 2 (over x), attn: 4 (over y, core), expert: 4 (over z).
Axes of the slice: x: 2, y: 2, z: 4, core: 2. Of those that a mesh axis runs over, the one named last changes fastest.
Arguments:
- tokens: bfloat16 [1024, 4096], P(('groups', 'attn'), 'expert'), parts along dimension 0, may hold values from -6 to 6
- expert_ids: int32 [1024, 8], P(('groups', 'attn')), parts along dimension 0, may hold values from 0 to 15, all different within a row; in each aligned block of 128 rows (0 to 127, 128 to 255, ...) at most 128 rows name the same one
- gate_weight: bfloat16 [1024, 8], P(('groups', 'attn')), parts along dimension 0, may hold values from 0.049804688 to 0.29882812
- w_gate: bfloat16 [16, 4096, 768], P('attn', 'expert'), may hold values from -0.09375 to 0.09375
- w_up: bfloat16 [16, 4096, 768], P('attn', 'expert'), may hold values from -0.09375 to 0.09375
- w_down: bfloat16 [16, 768, 4096], P('attn', None, 'expert'), may hold values from -0.21875 to 0.21875
- query: bfloat16 [64, 64, 128], P(('groups', 'attn', 'expert')), parts along dimension 0, may hold values from -100 to 100
- cache_k: bfloat16 [64, 768, 4, 128], P(('groups', 'attn', 'expert')), parts along dimension 0, may hold values from -6 to 6
- cache_v: bfloat16 [64, 768, 4, 128], P(('groups', 'attn', 'expert')), parts along dimension 0, may hold values from -6 to 6
- lengths: int32 [64], P(('groups', 'attn', 'expert')), parts along dimension 0, may hold values from 2 to 768, as said below
Outputs:
- moe_out: bfloat16 [1024, 4096], P(('groups', 'attn'), 'expert'), parts along dimension 0
- attn_out: bfloat16 [64, 8192], P(('groups', 'attn', 'expert')), parts along dimension 0
There are 2 independent parts, one for each index of `groups`. A program takes and returns all parts, laid end to end along the dimension named above; an argument that names none is the same for every part. Nothing has to cross between parts.
Inputs may be any that keep to these rules, and one draw needn't show every extreme that they name: `expert_ids`: each row names 8 different experts. In the rows of one index of attn (aligned blocks of 128 rows) no expert is named by more than 128 rows, and in some block some expert by exactly 128. `lengths`: some sequence has all 768 positions live.
All inputs are finite; a program needn't handle non-finite values.
Results may differ from a plain program's by a relative error of at most 0.025.
Values may be sent and summed in bfloat16 or wider, within the bound.
A program may use at most 64 MiB of HBM per device.

v0:
```python
import jax
import jax.numpy as jnp
from jax import lax
from jax.sharding import PartitionSpec as P


def member_table(expert_ids, experts):
    wanted = jnp.arange(experts, dtype=jnp.int32)
    return jnp.any(expert_ids[:, :, None] == wanted[None, None, :], axis=1).astype(jnp.int32)


def pad_rows(values):
    feat_width = values.shape[-1]
    flat_rows = values.reshape(-1, feat_width)
    return jnp.concatenate([flat_rows, jnp.zeros((1, feat_width), values.dtype)], axis=0)


def return_slots(results, starts_in, kept_in, slot_count):
    local_experts = results.shape[0]
    capacity = results.shape[1]
    slot_ids = jnp.arange(slot_count, dtype=jnp.int32)[None, None, :]
    column = jnp.arange(local_experts, dtype=jnp.int32)[None, :, None]
    row_index = column * capacity + starts_in[:, :, None] + slot_ids
    row_index = jnp.where(slot_ids < kept_in[:, :, None], row_index, local_experts * capacity)
    return pad_rows(results)[row_index]


def grouped_attention(query, cache_k, cache_v, lengths):
    seq_count, head_total, head_size = query.shape
    context = cache_k.shape[1]
    kv_count = cache_k.shape[2]
    grouped = query.reshape(seq_count, kv_count, head_total // kv_count, head_size)
    scores = jnp.einsum(
        "skgd,slkd->skgl", grouped, cache_k, preferred_element_type=jnp.float32
    ) * head_size ** (-0.5)
    live_mask = (
        lax.broadcasted_iota(jnp.int32, (seq_count, 1, 1, context), 3)
        < lengths[:, None, None, None]
    )
    masked = jnp.where(live_mask, scores, -jnp.inf)
    row_peak = jnp.max(masked, axis=3, keepdims=True)
    weighted = jnp.exp(masked - row_peak)
    denominator = jnp.sum(weighted, axis=3, keepdims=True)
    prob_bf = (weighted / denominator).astype(jnp.bfloat16)
    attended = jnp.einsum("skgl,slkd->skgd", prob_bf, cache_v, preferred_element_type=jnp.float32)
    return attended.reshape(seq_count, head_total * head_size).astype(jnp.bfloat16)


def body(tokens, expert_ids, gate_weight, w_gate, w_up, w_down, query, cache_k, cache_v, lengths):
    tok_rows, feat_width = tokens.shape
    top_count = expert_ids.shape[1]
    local_experts = w_gate.shape[0]
    ffn_width = w_gate.shape[2]
    attn_count = lax.axis_size("attn")
    experts = local_experts * attn_count
    capacity = tok_rows * top_count // local_experts
    slot_count = min(tok_rows, 3 * tok_rows * top_count // experts)
    member = member_table(expert_ids, experts)
    local_rank = jnp.cumsum(member, axis=0, dtype=jnp.int32) - member
    whole_ids = None
    whole_tokens, whole_ids, whole_gates = (
        lax.all_gather(tokens, "attn", axis=0, tiled=True),
        lax.all_gather(expert_ids, "attn", axis=0, tiled=True),
        lax.all_gather(gate_weight, "attn", axis=0, tiled=True),
    )
    all_rows = whole_tokens.shape[0]
    whole_member = member_table(whole_ids, experts)
    all_counts = jnp.sum(
        whole_member.reshape(attn_count, tok_rows, experts), axis=1, dtype=jnp.int32
    )
    src_offsets = jnp.cumsum(all_counts, axis=0, dtype=jnp.int32) - all_counts
    src_kept = jnp.clip(capacity - src_offsets, 0, all_counts)
    my_index = lax.axis_index("attn")
    offsets = lax.dynamic_index_in_dim(src_offsets, my_index, 0, keepdims=False)
    position = offsets[None, :] + local_rank
    starts_in = lax.dynamic_slice_in_dim(src_offsets, my_index * local_experts, local_experts, 1)
    kept_in = lax.dynamic_slice_in_dim(src_kept, my_index * local_experts, local_experts, 1)
    my_member = lax.dynamic_slice_in_dim(whole_member, my_index * local_experts, local_experts, 1)
    queue_place = jnp.cumsum(my_member, axis=0, dtype=jnp.int32) - my_member
    pack_target = jnp.where(
        (my_member > 0) & (queue_place < capacity),
        jnp.arange(local_experts, dtype=jnp.int32)[None, :] * capacity + queue_place,
        local_experts * capacity,
    )
    holders = jnp.broadcast_to(
        jnp.arange(all_rows, dtype=jnp.int32)[:, None], (all_rows, local_experts)
    )
    pack_index = (
        jnp.full((local_experts * capacity,), all_rows, jnp.int32)
        .at[pack_target.reshape(-1)]
        .set(holders.reshape(-1), mode="drop")
    )
    packed = pad_rows(whole_tokens)[pack_index].reshape(local_experts, capacity, feat_width)
    gate_part = jnp.einsum("jrd,jdf->jrf", packed, w_gate, preferred_element_type=jnp.float32)
    up_part = jnp.einsum("jrd,jdf->jrf", packed, w_up, preferred_element_type=jnp.float32)
    both_parts = jnp.concatenate([gate_part, up_part], axis=2)
    both_sums = lax.psum(both_parts.astype(jnp.bfloat16), "expert").astype(jnp.float32)
    hidden = (jax.nn.silu(both_sums[:, :, :ffn_width]) * both_sums[:, :, ffn_width:]).astype(
        jnp.bfloat16
    )
    results = jnp.einsum("jrf,jfd->jrd", hidden, w_down, preferred_element_type=jnp.float32).astype(
        jnp.bfloat16
    )
    back_rows = return_slots(results, starts_in, kept_in, slot_count)
    returned = lax.all_to_all(back_rows, "attn", split_axis=0, concat_axis=0, tiled=True)
    slot_of = jnp.take_along_axis(local_rank, expert_ids, axis=1)
    place_of = jnp.take_along_axis(position, expert_ids, axis=1)
    keep_mask = place_of < capacity
    picked = returned.reshape(experts * slot_count, feat_width)[expert_ids * slot_count + slot_of]
    factor = jnp.where(keep_mask, gate_weight.astype(jnp.float32), 0.0)
    moe_out = jnp.sum(factor[:, :, None] * picked.astype(jnp.float32), axis=1).astype(jnp.bfloat16)
    attn_out = grouped_attention(query, cache_k, cache_v, lengths)
    return (moe_out, attn_out)


def solution(mesh):
    return jax.shard_map(
        body,
        mesh=mesh,
        in_specs=(
            P(("groups", "attn"), "expert"),
            P(("groups", "attn"), None),
            P(("groups", "attn"), None),
            P("attn", "expert", None),
            P("attn", "expert", None),
            P("attn", None, "expert"),
            P(("groups", "attn", "expert"), None, None),
            P(("groups", "attn", "expert"), None, None, None),
            P(("groups", "attn", "expert"), None, None, None),
            P(("groups", "attn", "expert")),
        ),
        out_specs=(P(("groups", "attn"), "expert"), P(("groups", "attn", "expert"), None)),
        check_vma=False,
    )
```

profile of v0, /device:TPU:0, one launch (start us, length us, event | category | flops | bytes accessed | tf_op | source)
XLA Modules:
  0.0 263.3 jit_solution(12744865341679624601)
XLA Ops:
  7.2 0.7 all-gather.2.cloned.1.call-update
  8.0 6.4 %all_gather.6 = s32[512,8]{0,1:T(8,128)S(1)} all-gather(s32[128,8]{0,1:T(8,128)} %param.13), channel_id=1, replica_groups=mesh['groups'=2,'attn'=4,'expert'=4] {'attn'}, dimensions={0}, use_global_device_ids=true | all-gather | bytes 20480 | tf_op jit(solution)/shard_map/all_gather | solution.py:63
  14.5 1.2 reduce-window.6
  15.7 0.2 slice_reduce_fusion
  15.9 0.2 reduce-window.9
  16.4 0.2 reshape.138
  16.6 0.2 reshape.186
  16.8 8.0 %scatter_custom_fusion = s32[1024]{0:T(1024)S(1)} fusion(s32[2048]{0:T(1024)S(1)} %bitcast.56, s32[2048]{0:T(1024)S(1)} %reshape.186, s32[]{:T(128)} %constant.34.clone.1), kind=kCustom, calls=%fused_computation.57 | custom fusion | bytes 4100 | tf_op jit(solution)/shard_map/scatter | solution.py:91
  24.9 4.2 %all-gather.2.cloned.1.call-done = bf16[512,1024]{1,0:T(8,128)(2,1)} async-done(((bf16[128,1024]{1,0:T(8,128)(2,1)}), bf16[512,1024]{1,0:T(8,128)(2,1)}) %all-gather.2.cloned.1.call-update) | async-done | bytes 1048592 | tf_op jit(solution)/shard_map/all_gather | solution.py:62
  29.0 1.3 concatenate.10
  30.3 5.4 %gather_fusion = bf16[1024,1024]{1,0:T(8,128)(2,1)} fusion(bf16[513,1024]{1,0:T(8,128)(2,1)S(1)} %concatenate.10, s32[1024]{0:T(1024)S(1)} %fusion.24), kind=kCustom, calls=%fused_computation.2 | custom fusion | bytes 4198400 | tf_op jit(solution)/shard_map/gather | solution.py:93
  35.7 5.4 %convolution_convert_fusion.1 = bf16[4,256,768]{2,1,0:T(8,128)(2,1)S(1)} fusion(bf16[4,256,1024]{2,1,0:T(8,128)(2,1)} %bitcast.48, bf16[4,1024,768]{2,1,0:T(8,128)(2,1)} %param.16), kind=kOutput, calls=%fused_computation.13 | convolution fusion | flops 1611399168 | bytes 9961472 | tf_op jit(solution)/shard_map/jrd,jdf->jrf/dot_general | solution.py:95
  41.0 4.6 %convolution_convert_fusion.2 = bf16[4,256,768]{2,1,0:T(8,128)(2,1)S(1)} fusion(bf16[4,256,1024]{2,1,0:T(8,128)(2,1)S(1)} %bitcast.49, bf16[4,1024,768]{2,1,0:T(8,128)(2,1)} %param.15), kind=kOutput, calls=%fused_computation.14 | convolution fusion | flops 1611399168 | bytes 9961472 | tf_op jit(solution)/shard_map/jrd,jdf->jrf/dot_general | solution.py:94
  45.6 2.0 pad_maximum_fusion
  47.6 0.3 reduce_sum.27
  48.5 120.3 %all-reduce.4.cloned.1.call-done = bf16[4,256,1536]{2,1,0:T(8,128)(2,1)} async-done(((bf16[4,256,1536]{2,1,0:T(8,128)(2,1)}), bf16[4,256,1536]{2,1,0:T(8,128)(2,1)}) %all-reduce.4.cloned.1.call-update) | async-done | bytes 3145744 | tf_op jit(solution)/shard_map/psum | solution.py:97
  168.8 2.7 %convert_element_type.45 = f32[4,256,1536]{2,1,0:T(8,128)S(1)} convert(bf16[4,256,1536]{2,1,0:T(8,128)(2,1)} %all-reduce.4.cloned.1.call-done) | non-fusion elementwise | flops 1572864 | bytes 9437184 | tf_op jit(solution)/shard_map/convert_element_type | solution.py:97
  171.6 4.9 %convolution_convert_fusion = bf16[4,256,1024]{2,1,0:T(8,128)(2,1)S(1)} fusion(bf16[4,768,1024]{2,1,0:T(8,128)(2,1)} %param.17, f32[4,256,1536]{2,1,0:T(8,128)S(1)} %convert_element_type.45), kind=kOutput, calls=%fused_computation.12 | convolution fusion | flops 1616379904 | bytes 14680064 | tf_op jit(solution)/shard_map/jrf,jfd->jrd/dot_general | solution.py:101
  176.4 1.5 concatenate.12
  178.0 12.9 %gather_fusion.1 = bf16[2048,1024]{1,0:T(8,128)(2,1)} fusion(bf16[1025,1024]{1,0:T(8,128)(2,1)} %concatenate.12, s32[2048]{0:T(1024)S(1)} %broadcast_clamp_fusion), kind=kCustom, calls=%fused_computation.3 | custom fusion | bytes 8396800 | tf_op jit(solution)/shard_map/gather | solution.py:25
  190.8 5.2 %all-to-all-start = ((bf16[4,4,128,1024]{3,2,1,0:T(8,128)(2,1)}), bf16[4,4,128,1024]{3,2,1,0:T(8,128)(2,1)}, u32[]{:S(2)}, u32[]{:S(2)}) async-start(bf16[4,4,128,1024]{3,2,1,0:T(8,128)(2,1)} %bitcast.47), calls=%async_computation | async-start | bytes 8388608 | tf_op jit(solution)/shard_map/all_to_all | solution.py:105
  196.2 0.2 reduce_window_sum.38
  196.5 0.2 dynamic-slice_reduce_fusion
  196.7 7.1 %gather_fusion.4 = s32[1024]{0:T(1024)S(1)} fusion(s32[128,16]{1,0:T(8,128)S(1)} %get-tuple-element.4, s32[1024]{0:T(1024)S(1)} %reshape.206), kind=kCustom, calls=%fused_computation.1.clone | custom fusion | bytes 16384 | tf_op jit(solution)/shard_map/jit(take_along_axis)/gather | solution.py:106
  204.2 7.1 %gather_fusion.3 = s32[1024]{0:T(1024)S(1)} fusion(s32[128,16]{1,0:T(8,128)S(1)} %get-tuple-element.3, s32[1024]{0:T(1024)S(1)} %reshape.206), kind=kCustom, calls=%fused_computation.clone | custom fusion | bytes 16384 | tf_op jit(solution)/shard_map/jit(take_along_axis)/gather | solution.py:107
  211.7 0.5 fusion.14
  212.2 0.2 fusion.29
  212.4 1.8 fusion.17
  214.2 0.7 copy.127
  214.9 29.1 %all-to-all-done = bf16[4,4,128,1024]{3,2,1,0:T(8,128)(2,1)} async-done(((bf16[4,4,128,1024]{3,2,1,0:T(8,128)(2,1)}), bf16[4,4,128,1024]{3,2,1,0:T(8,128)(2,1)}, u32[]{:S(2)}, u32[]{:S(2)}) %all-to-all-start) | async-done | bytes 4194336 | tf_op jit(solution)/shard_map/all_to_all | solution.py:105
  244.0 8.8 %gather_fusion.2 = bf16[1024,1024]{1,0:T(8,128)(2,1)} fusion(bf16[2048,1024]{1,0:T(8,128)(2,1)} %bitcast.8, s32[1024]{0:T(1024)S(1)} %broadcast_clamp_fusion.1), kind=kCustom, calls=%fused_computation.4 | custom fusion | bytes 4198400 | tf_op jit(solution)/shard_map/gather | solution.py:109
  252.8 3.7 %fusion.1 = bf16[128,1024]{1,0:T(8,128)(2,1)} fusion(bf16[1024,1024]{1,0:T(8,128)(2,1)} %gather_fusion.2, f32[128,8]{1,0:T(8,128)S(1)} %copy.102), kind=kLoop, calls=%fused_computation.8 | loop fusion | flops 3014656 | bytes 2363392 | tf_op jit(solution)/shard_map/reduce_sum | solution.py:111
  (52 shorter events, 2.1 us)
Async XLA Ops:
  7.2 204.5 %copy-start = (bf16[2,768,4,128]{3,2,1,0:T(4,128)(2,1)S(1)}, bf16[2,768,4,128]{3,2,1,0:T(4,128)(2,1)}, u32[]{:S(2)}) copy-start(bf16[2,768,4,128]{3,2,1,0:T(4,128)(2,1)} %param.19) | copy-start | bytes 4718596
  7.2 21.8 %all-gather.2.cloned.1.call-start = ((), (), s32[]{:S(2)}) async-start(), calls=%async_computation.1 | async-start | bytes 1310720 | tf_op jit(solution)/shard_map/all_gather | solution.py:62
  7.9 160.9 %all-reduce.4.cloned.1.call-start = ((), (), s32[]{:S(2)}) async-start(), calls=%async_computation.2 | async-start | bytes 6291456 | tf_op jit(solution)/shard_map/psum | solution.py:97
  35.7 5.4 %copy-start.1 = (bf16[1024,1024]{1,0:T(8,128)(2,1)S(1)}, bf16[1024,1024]{1,0:T(8,128)(2,1)}, u32[]{:S(2)}) copy-start(bf16[1024,1024]{1,0:T(8,128)(2,1)} %gather_fusion) | copy-start | bytes 6291460
  190.8 5.2 %copy-start.2 = (s32[128,8]{0,1:T(8,128)S(1)}, s32[128,8]{0,1:T(8,128)}, u32[]{:S(2)}) copy-start(s32[128,8]{0,1:T(8,128)} %param.13) | copy-start | bytes 12292
  190.8 53.2 %all-to-all-start = ((bf16[4,4,128,1024]{3,2,1,0:T(8,128)(2,1)}), bf16[4,4,128,1024]{3,2,1,0:T(8,128)(2,1)}, u32[]{:S(2)}, u32[]{:S(2)}) async-start(bf16[4,4,128,1024]{3,2,1,0:T(8,128)(2,1)} %bitcast.47), calls=%async_computation | async-start | bytes 8388608 | tf_op jit(solution)/shard_map/all_to_all | solution.py:105
  204.2 7.3 %copy-start.4 = (bf16[128,8]{0,1:T(8,128)(2,1)S(1)}, bf16[128,8]{0,1:T(8,128)(2,1)}, u32[]{:S(2)}) copy-start(bf16[128,8]{0,1:T(8,128)(2,1)} %param.14) | copy-start | bytes 6148
  204.2 7.4 %copy-start.5 = (s32[2]{0:T(128)S(1)}, s32[2]{0:T(128)}, u32[]{:S(2)}) copy-start(s32[2]{0:T(128)} %param.21) | copy-start | bytes 28
  204.2 7.4 %copy-start.3 = (bf16[2,64,128]{2,1,0:T(8,128)(2,1)S(1)}, bf16[2,64,128]{2,1,0:T(8,128)(2,1)}, u32[]{:S(2)}) copy-start(bf16[2,64,128]{2,1,0:T(8,128)(2,1)} %param.18) | copy-start | bytes 98308
Sparse Core Ops, SparseCore 0:
  9.5 19.4 all-gather.1
  47.7 121.0 all-reduce.3
where the time goes:
time: 264 us; the launch traced here: 263 us
  waiting for transfers between devices  154 us (58%)
  local copies, waits for them, and re-layouts  54.7 us (21%)
  matrix products  17.1 us (6%)
  between operations  14.3 us (5%)
  other arithmetic  11.2 us (4%)
  blocking collectives  6.41 us (2%)
  starting transfers between devices  5.25 us (2%)
    psum x1, waiting for transfers between devices, body(): lax.psum(both_parts.astype(jnp.bfloat16), 'expert').astype(jnp.float32)  120 us
    all_to_all x1, waiting for transfers between devices, body(): lax.all_to_all(back_rows, 'attn', split_axis=0, concat_axis=0, tiled=True)  29.1 us
    gather x1, local copies, waits for them, and re-layouts, return_slots(): return pad_rows(results)[row_index]  12.9 us
    gather x1, local copies, waits for them, and re-layouts, body(): returned.reshape(experts * slot_count, feat_width)  8.78 us
    scatter x1, local copies, waits for them, and re-layouts, body(): pack_index = jnp.full((local_experts * capacity,), all_rows, jnp.int32).a...  8.04 us
    gather x5, local copies, waits for them, and re-layouts, body(): place_of = jnp.take_along_axis(position, expert_ids, axis=1)  7.39 us
    gather x3, local copies, waits for them, and re-layouts, body(): slot_of = jnp.take_along_axis(local_rank, expert_ids, axis=1)  7.2 us
    all_gather x1, blocking collectives, body(): lax.all_gather(expert_ids, 'attn', axis=0, tiled=True)  6.41 us
  transfers between devices with their start and end apart: 3, of which 3 were waited for; matrix products, arithmetic and copies ran while one was open for 11% of the time, Pallas kernels for 0%

commit v1 on v0

--- a/solution.py
+++ b/solution.py
@@ -1,7 +1,16 @@
+import functools
 import jax
 import jax.numpy as jnp
 from jax import lax
 from jax.sharding import PartitionSpec as P
+
+
+def clear_samples_all_in(frame_in, named_axis):
+    next_value = jnp.sum(lax.all_gather(frame_in, axis_name=named_axis), axis=0)
+    return next_value
+
+
+_lead_heads = functools.partial(clear_samples_all_in, named_axis="expert")
 
 
 def member_table(expert_ids, experts):
@@ -94,7 +103,7 @@
     gate_part = jnp.einsum("jrd,jdf->jrf", packed, w_gate, preferred_element_type=jnp.float32)
     up_part = jnp.einsum("jrd,jdf->jrf", packed, w_up, preferred_element_type=jnp.float32)
     both_parts = jnp.concatenate([gate_part, up_part], axis=2)
-    both_sums = lax.psum(both_parts.astype(jnp.bfloat16), "expert").astype(jnp.float32)
+    both_sums = _lead_heads(both_parts.astype(jnp.bfloat16)).astype(jnp.float32)
     hidden = (jax.nn.silu(both_sums[:, :, :ffn_width]) * both_sums[:, :, ffn_width:]).astype(
         jnp.bfloat16
     )

time: 264 us -> 370 us (1.40)
  waiting for transfers between devices: 154 us -> 251 us
  other arithmetic: 11.2 us -> 20.3 us
    all_gather x0 -> x1, waiting for transfers between devices: none -> 217 us  [clear_samples_all_in(): next_value = jnp.sum(lax.all_gather(frame_in, axis_name=named_axis), axis=0)]
    psum x1 -> x0, waiting for transfers between devices: 120 us -> none  [body(): lax.psum(both_parts.astype(jnp.bfloat16), 'expert').astype(jnp.float32)]
    reduce_sum x0 -> x1, other arithmetic: none -> 9.15 us  [clear_samples_all_in(): next_value = jnp.sum(lax.all_gather(frame_in, axis_name=named_axis), axis=0)]
  transfers between devices with their start and end apart: 3 -> 3, of which waited for: 3 -> 3; matrix products, arithmetic and copies ran while one was open for 11% -> 8% of each run, Pallas kernels for 0% -> 0%
where the time goes in v1:
time: 370 us
  waiting for transfers between devices  251 us (68%)
  local copies, waits for them, and re-layouts  54.7 us (15%)
  other arithmetic  20.3 us (5%)
  matrix products  17.1 us (5%)
  between operations  14.3 us (4%)
  blocking collectives  6.41 us (2%)
  starting transfers between devices  5.25 us (1%)
    all_gather x1, waiting for transfers between devices, clear_samples_all_in(): next_value = jnp.sum(lax.all_gather(frame_in, axis_name=named_axis), axis=0)  217 us
    all_to_all x1, waiting for transfers between devices, body(): lax.all_to_all(back_rows, 'attn', split_axis=0, concat_axis=0, tiled=True)  29.1 us
    gather x1, local copies, waits for them, and re-layouts, return_slots(): return pad_rows(results)[row_index]  12.9 us
    reduce_sum x1, other arithmetic, clear_samples_all_in(): next_value = jnp.sum(lax.all_gather(frame_in, axis_name=named_axis), axis=0)  9.15 us
    gather x1, local copies, waits for them, and re-layouts, body(): returned.reshape(experts * slot_count, feat_width)  8.78 us
    scatter x1, local copies, waits for them, and re-layouts, body(): pack_index = jnp.full((local_experts * capacity,), all_rows, jnp.int32).a...  8.04 us
  transfers between devices with their start and end apart: 3, of which 3 were waited for; matrix products, arithmetic and copies ran while one was open for 8% of the time, Pallas kernels for 0%

profile of v1, /device:TPU:0, one launch (start us, length us, event | category | flops | bytes accessed | tf_op | source)
XLA Modules:
  0.0 369.5 jit_solution(14124152021767163328)
XLA Ops:
  7.2 0.7 all-gather.3.cloned.1.call-update
  8.0 6.4 %all_gather.10 = s32[512,8]{0,1:T(8,128)S(1)} all-gather(s32[128,8]{0,1:T(8,128)} %param.13), channel_id=1, replica_groups=mesh['groups'=2,'attn'=4,'expert'=4] {'attn'}, dimensions={0}, use_global_device_ids=true | all-gather | bytes 20480 | tf_op jit(solution)/shard_map/all_gather | solution.py:72
  14.5 1.2 reduce-window.6
  15.7 0.2 slice_reduce_fusion
  15.9 0.2 reduce-window.9
  16.4 0.2 reshape.169
  16.8 8.0 %scatter_custom_fusion = s32[1024]{0:T(1024)S(1)} fusion(s32[2048]{0:T(1024)S(1)} %bitcast.60, s32[2048]{0:T(1024)S(1)} %reshape.217, s32[]{:T(128)} %constant.34.clone.1), kind=kCustom, calls=%fused_computation.59 | custom fusion | bytes 4100 | tf_op jit(solution)/shard_map/scatter | solution.py:100
  24.9 4.2 %all-gather.3.cloned.1.call-done = bf16[512,1024]{1,0:T(8,128)(2,1)} async-done(((bf16[128,1024]{1,0:T(8,128)(2,1)}), bf16[512,1024]{1,0:T(8,128)(2,1)}) %all-gather.3.cloned.1.call-update) | async-done | bytes 1048592 | tf_op jit(solution)/shard_map/all_gather | solution.py:71
  29.0 1.3 concatenate.21
  30.3 5.4 %gather_fusion = bf16[1024,1024]{1,0:T(8,128)(2,1)} fusion(bf16[513,1024]{1,0:T(8,128)(2,1)S(1)} %concatenate.21, s32[1024]{0:T(1024)S(1)} %fusion.26), kind=kCustom, calls=%fused_computation.2 | custom fusion | bytes 4198400 | tf_op jit(solution)/shard_map/gather | solution.py:102
  35.7 5.4 %fusion.10 = bf16[1,4,256,768]{3,2,1,0:T(8,128)(2,1)S(1)} fusion(bf16[4,256,1024]{2,1,0:T(8,128)(2,1)} %bitcast.52, bf16[4,1024,768]{2,1,0:T(8,128)(2,1)} %param.16), kind=kOutput, calls=%fused_computation.21 | convolution fusion | flops 1611399168 | bytes 9961472 | tf_op jit(solution)/shard_map/jrd,jdf->jrf/dot_general | solution.py:104
  41.0 4.6 %fusion.9 = bf16[1,4,256,768]{3,2,1,0:T(8,128)(2,1)S(1)} fusion(bf16[4,256,1024]{2,1,0:T(8,128)(2,1)S(1)} %bitcast.53, bf16[4,1024,768]{2,1,0:T(8,128)(2,1)} %param.15), kind=kOutput, calls=%fused_computation.20 | convolution fusion | flops 1611399168 | bytes 9961472 | tf_op jit(solution)/shard_map/jrd,jdf->jrf/dot_general | solution.py:103
  45.6 1.9 pad_maximum_fusion
  47.6 0.3 reduce_sum.39
  48.5 217.5 %all-gather.5.cloned.1.call-done = bf16[4,4,256,1536]{3,2,1,0:T(8,128)(2,1)} async-done(((bf16[1,4,256,1536]{3,2,1,0:T(8,128)(2,1)}), bf16[4,4,256,1536]{3,2,1,0:T(8,128)(2,1)}) %all-gather.5.cloned.1.call-update) | async-done | bytes 12582928 | tf_op jit(solution)/shard_map/all_gather | solution.py:9
  265.9 9.2 %reduce_sum.40 = bf16[4,256,1536]{2,1,0:T(8,128)(2,1)} reduce(bf16[4,4,256,1536]{3,2,1,0:T(8,128)(2,1)} %all-gather.5.cloned.1.call-done, bf16[]{:T(256)} %constant.19.clone.1), dimensions={0}, to_apply=%region_8.10 | reduce | flops 4718592 | bytes 15728642 | tf_op jit(solution)/shard_map/reduce_sum | solution.py:9
  275.1 2.7 convert_element_type.54
  277.8 4.8 %convolution_convert_fusion = bf16[4,256,1024]{2,1,0:T(8,128)(2,1)S(1)} fusion(bf16[4,768,1024]{2,1,0:T(8,128)(2,1)} %param.17, f32[4,256,1536]{2,1,0:T(8,128)S(1)} %convert_element_type.54), kind=kOutput, calls=%fused_computation.12 | convolution fusion | flops 1616379904 | bytes 14680064 | tf_op jit(solution)/shard_map/jrf,jfd->jrd/dot_general | solution.py:110
  282.7 1.5 concatenate.25
  284.2 12.9 %gather_fusion.1 = bf16[2048,1024]{1,0:T(8,128)(2,1)} fusion(bf16[1025,1024]{1,0:T(8,128)(2,1)} %concatenate.25, s32[2048]{0:T(1024)S(1)} %broadcast_clamp_fusion), kind=kCustom, calls=%fused_computation.3 | custom fusion | bytes 8396800 | tf_op jit(solution)/shard_map/gather | solution.py:34
  297.1 5.2 %all-to-all-start = ((bf16[4,4,128,1024]{3,2,1,0:T(8,128)(2,1)}), bf16[4,4,128,1024]{3,2,1,0:T(8,128)(2,1)}, u32[]{:S(2)}, u32[]{:S(2)}) async-start(bf16[4,4,128,1024]{3,2,1,0:T(8,128)(2,1)} %bitcast.51), calls=%async_computation | async-start | bytes 8388608 | tf_op jit(solution)/shard_map/all_to_all | solution.py:114
  302.4 0.2 reduce_window_sum.38
  302.8 0.2 dynamic-slice_reduce_fusion
  303.0 7.1 %gather_fusion.4 = s32[1024]{0:T(1024)S(1)} fusion(s32[128,16]{1,0:T(8,128)S(1)} %get-tuple-element.4, s32[1024]{0:T(1024)S(1)} %reshape.237), kind=kCustom, calls=%fused_computation.1.clone | custom fusion | bytes 16384 | tf_op jit(solution)/shard_map/jit(take_along_axis)/gather | solution.py:115
  310.5 7.1 %gather_fusion.3 = s32[1024]{0:T(1024)S(1)} fusion(s32[128,16]{1,0:T(8,128)S(1)} %get-tuple-element.3, s32[1024]{0:T(1024)S(1)} %reshape.237), kind=kCustom, calls=%fused_computation.clone | custom fusion | bytes 16384 | tf_op jit(solution)/shard_map/jit(take_along_axis)/gather | solution.py:116
  317.9 0.5 fusion.16
  318.4 0.2 fusion.31
  318.7 1.8 fusion.19
  320.5 0.7 copy.148
  321.2 29.1 %all-to-all-done = bf16[4,4,128,1024]{3,2,1,0:T(8,128)(2,1)} async-done(((bf16[4,4,128,1024]{3,2,1,0:T(8,128)(2,1)}), bf16[4,4,128,1024]{3,2,1,0:T(8,128)(2,1)}, u32[]{:S(2)}, u32[]{:S(2)}) %all-to-all-start) | async-done | bytes 4194336 | tf_op jit(solution)/shard_map/all_to_all | solution.py:114
  350.3 8.8 %gather_fusion.2 = bf16[1024,1024]{1,0:T(8,128)(2,1)} fusion(bf16[2048,1024]{1,0:T(8,128)(2,1)} %bitcast.10, s32[1024]{0:T(1024)S(1)} %broadcast_clamp_fusion.1), kind=kCustom, calls=%fused_computation.4 | custom fusion | bytes 4198400 | tf_op jit(solution)/shard_map/gather | solution.py:118
  359.0 3.7 fusion.1
  (53 shorter events, 2.3 us)
Async XLA Ops:
  7.2 310.8 %copy-start = (bf16[2,768,4,128]{3,2,1,0:T(4,128)(2,1)S(1)}, bf16[2,768,4,128]{3,2,1,0:T(4,128)(2,1)}, u32[]{:S(2)}) copy-start(bf16[2,768,4,128]{3,2,1,0:T(4,128)(2,1)} %param.19) | copy-start | bytes 4718596
  7.2 21.8 %all-gather.3.cloned.1.call-start = ((), (), s32[]{:S(2)}) async-start(), calls=%async_computation.1 | async-start | bytes 1310720 | tf_op jit(solution)/shard_map/all_gather | solution.py:71
  7.9 258.0 %all-gather.5.cloned.1.call-start = ((), (), s32[]{:S(2)}) async-start(), calls=%async_computation.2 | async-start | bytes 15728640 | tf_op jit(solution)/shard_map/all_gather | solution.py:9
  35.7 5.4 %copy-start.1 = (bf16[1024,1024]{1,0:T(8,128)(2,1)S(1)}, bf16[1024,1024]{1,0:T(8,128)(2,1)}, u32[]{:S(2)}) copy-start(bf16[1024,1024]{1,0:T(8,128)(2,1)} %gather_fusion) | copy-start | bytes 6291460
  297.1 5.2 %copy-start.2 = (s32[128,8]{0,1:T(8,128)S(1)}, s32[128,8]{0,1:T(8,128)}, u32[]{:S(2)}) copy-start(s32[128,8]{0,1:T(8,128)} %param.13) | copy-start | bytes 12292
  297.1 53.2 %all-to-all-start = ((bf16[4,4,128,1024]{3,2,1,0:T(8,128)(2,1)}), bf16[4,4,128,1024]{3,2,1,0:T(8,128)(2,1)}, u32[]{:S(2)}, u32[]{:S(2)}) async-start(bf16[4,4,128,1024]{3,2,1,0:T(8,128)(2,1)} %bitcast.51), calls=%async_computation | async-start | bytes 8388608 | tf_op jit(solution)/shard_map/all_to_all | solution.py:114
  310.5 7.3 %copy-start.4 = (bf16[128,8]{0,1:T(8,128)(2,1)S(1)}, bf16[128,8]{0,1:T(8,128)(2,1)}, u32[]{:S(2)}) copy-start(bf16[128,8]{0,1:T(8,128)(2,1)} %param.14) | copy-start | bytes 6148
  310.5 7.4 %copy-start.5 = (s32[2]{0:T(128)S(1)}, s32[2]{0:T(128)}, u32[]{:S(2)}) copy-start(s32[2]{0:T(128)} %param.21) | copy-start | bytes 28
  310.5 7.4 %copy-start.3 = (bf16[2,64,128]{2,1,0:T(8,128)(2,1)S(1)}, bf16[2,64,128]{2,1,0:T(8,128)(2,1)}, u32[]{:S(2)}) copy-start(bf16[2,64,128]{2,1,0:T(8,128)(2,1)} %param.18) | copy-start | bytes 98308
Sparse Core Ops, SparseCore 0:
  9.5 19.4 all-gather.2
  47.7 218.1 all-gather.4
